TPU v7x, 128 devices: a whole 4x4x4 slice. The times are simulated.
128 devices in a mesh: ka: 32 (over z, y, core), col: 4 (over x).
Axes of the slice: x: 4, y: 4, z: 4, core: 2. Of those that a mesh axis runs over, the one named last changes fastest.
Arguments:
- hamiltonian: bfloat16 [1024, 2, 9216], P(('ka', 'col')), may hold values from -0.1875 to 0.1875
- eigvecs: bfloat16 [2048, 2, 96, 96], P('ka'), may hold values from -0.625 to 0.625
- spin: bfloat16 [2, 96, 96], replicated, may hold values from -0.059814453 to 0.059814453
- k_indices: int32 [2048, 3], P('ka'), may hold values from 0 to 63
- r_vectors: int32 [1024, 3], replicated, may hold values from -5 to 5, as said below
- degeneracy: int32 [1024], replicated, may hold values from 1 to 4
- fermi_level: float32 [1], replicated, may hold values from -0.5 to 0.5
Outputs:
- band_curvature: float32 [9, 96, 2048], P(None, None, ('ka', 'col'))
- conductivity: float32 [9, 96], replicated
Inputs may be any that keep to these rules, and one draw needn't show every extreme that they name: `r_vectors`: the 1024 lattice vectors are all distinct.
All inputs are finite; a program needn't handle non-finite values.
Results may differ from a plain program's by a relative error of at most 0.0085.
The roundings to bfloat16 on the way count: a program that leaves them out, or rounds other values in their place, can miss the bound.
Values may be sent and summed in bfloat16 or wider, within the bound.
No kernel may reach another device: no remote copies, remote signals or barrier semaphores. Data moves between devices by JAX's collectives and lax.ppermute only.
A program may use at most 128 MiB of HBM per device.

v0:
```python
import math
import jax
import jax.numpy as jnp
from jax import lax
from jax.sharding import PartitionSpec as P

WF = 96
GRID = 64
two_pi = 2.0 * math.pi
broadening = 0.5
smearing = 0.1


def sent_to_all(value, axis):
    copies = jnp.broadcast_to(value, (lax.axis_size(axis), *value.shape))
    return lax.all_to_all(copies, axis, split_axis=0, concat_axis=0, tiled=True)


def taken_together(value, axis):
    everything = sent_to_all(value, axis)
    return jnp.sum(everything, axis=0)


def phase_rows(kpoints, lattice, degrees, height):
    flat_index = jnp.arange(height, dtype=jnp.int32)
    vector_index = flat_index // 2
    halves = flat_index % 2
    lattice_rows = jnp.take(lattice, vector_index, axis=0)
    degree_rows = jnp.take(degrees, vector_index, axis=0)
    lattice_dot = jnp.mod(jnp.sum(kpoints[:, None, :] * lattice_rows[None, :, :], axis=-1), GRID)
    angles = lattice_dot.astype(jnp.float32) * (two_pi / GRID)
    cosine = jnp.cos(angles)
    sine_part = jnp.sin(angles)
    inverse = 1.0 / degree_rows.astype(jnp.float32)
    coords = lattice_rows.astype(jnp.float32) * inverse[:, None]
    real_part = jnp.stack(
        [
            cosine * inverse,
            -sine_part * coords[:, 0],
            -sine_part * coords[:, 1],
            -sine_part * coords[:, 2],
        ],
        axis=1,
    )
    imag_part = jnp.stack(
        [sine_part * inverse, cosine * coords[:, 0], cosine * coords[:, 1], cosine * coords[:, 2]],
        axis=1,
    )
    real_rows = (halves == 0)[None, None, :]
    top_rows = jnp.where(real_rows, real_part, -imag_part)
    low_rows = jnp.where(real_rows, imag_part, real_part)
    return jnp.stack([top_rows, low_rows], axis=2)


def rotate(operators, vectors):
    ops_re = operators[:, :, 0]
    ops_im = operators[:, :, 1]
    vec_re = vectors[:, 0]
    vec_im = vectors[:, 1]
    half_re = jnp.einsum(
        "kcij,kjm->kcim", ops_re, vec_re, preferred_element_type=jnp.float32
    ) - jnp.einsum("kcij,kjm->kcim", ops_im, vec_im, preferred_element_type=jnp.float32)
    half_im = jnp.einsum(
        "kcij,kjm->kcim", ops_re, vec_im, preferred_element_type=jnp.float32
    ) + jnp.einsum("kcij,kjm->kcim", ops_im, vec_re, preferred_element_type=jnp.float32)
    half_re = half_re.astype(jnp.bfloat16)
    half_im = half_im.astype(jnp.bfloat16)
    full_re = jnp.einsum(
        "kjn,kcjm->kcnm", vec_re, half_re, preferred_element_type=jnp.float32
    ) + jnp.einsum("kjn,kcjm->kcnm", vec_im, half_im, preferred_element_type=jnp.float32)
    full_im = jnp.einsum(
        "kjn,kcjm->kcnm", vec_re, half_im, preferred_element_type=jnp.float32
    ) - jnp.einsum("kjn,kcjm->kcnm", vec_im, half_re, preferred_element_type=jnp.float32)
    sym_re = (full_re + jnp.swapaxes(full_re, -1, -2)) * 0.5
    sym_im = (full_im - jnp.swapaxes(full_im, -1, -2)) * 0.5
    return jnp.stack([sym_re, sym_im], axis=2).astype(jnp.bfloat16)


def kubo(bloch_ops, spin_bloch, fermi_level):
    energy = jnp.diagonal(bloch_ops[:, 0, 0].astype(jnp.float32), axis1=-2, axis2=-1)
    velo_re = bloch_ops[:, 1:, 0].astype(jnp.float32)
    velo_im = bloch_ops[:, 1:, 1].astype(jnp.float32)
    spin_re = spin_bloch[:, 0].astype(jnp.float32)
    spin_im = spin_bloch[:, 1].astype(jnp.float32)
    prod_re = jnp.einsum("kij,kajm->kaim", spin_re, velo_re) - jnp.einsum(
        "kij,kajm->kaim", spin_im, velo_im
    )
    prod_im = jnp.einsum("kij,kajm->kaim", spin_re, velo_im) + jnp.einsum(
        "kij,kajm->kaim", spin_im, velo_re
    )
    cur_re = (prod_re + jnp.swapaxes(prod_re, -1, -2)) * 0.5
    cur_im = (prod_im - jnp.swapaxes(prod_im, -1, -2)) * 0.5
    energy_gap = energy[:, :, None] - energy[:, None, :]
    weight = 1.0 / (energy_gap * energy_gap + broadening * broadening)
    curvature = -2.0 * (
        jnp.einsum("kanm,kbmn,knm->kabn", cur_re, velo_im, weight)
        + jnp.einsum("kanm,kbmn,knm->kabn", cur_im, velo_re, weight)
    )
    occupation = 1.0 / (1.0 + jnp.exp((energy - fermi_level[0]) / smearing))
    weighted = jnp.einsum("kn,kabn->abn", occupation, curvature)
    return (curvature, weighted)


def on_device(hamiltonian, eigvecs, spin, k_indices, r_vectors, degeneracy, fermi_level):
    kcount = eigvecs.shape[0]
    col_count = lax.axis_size("col")
    quarter = kcount // col_count
    column = lax.axis_index("col")
    vectors = lax.dynamic_slice_in_dim(eigvecs, column * quarter, quarter, 0)
    flat_shard = hamiltonian.reshape(hamiltonian.shape[0] * 2, WF * WF)
    entry_width = WF * WF // col_count
    entry_slice = lax.all_to_all(flat_shard, "col", split_axis=1, concat_axis=0, tiled=True)
    segment = lax.all_gather(entry_slice, "ka", axis=0, tiled=True)
    height = segment.shape[0]
    phases = phase_rows(k_indices, r_vectors, degeneracy, height)
    phases = phases.reshape(kcount * 8, height).astype(jnp.bfloat16)
    summed = jnp.dot(phases, segment, preferred_element_type=jnp.float32)
    summed = summed.reshape(kcount, 4, 2, entry_width)
    own_entries = summed.astype(jnp.bfloat16)
    regrouped = lax.all_to_all(own_entries, "col", split_axis=0, concat_axis=3, tiled=True)
    interpolated = regrouped.reshape(quarter, 4, 2, WF, WF)
    bloch_ops = rotate(interpolated, vectors)
    spin_wide = spin.astype(jnp.float32)
    spin_sym = jnp.stack(
        [(spin_wide[0] + spin_wide[0].T) * 0.5, (spin_wide[1] - spin_wide[1].T) * 0.5]
    ).astype(jnp.bfloat16)
    spin_ops = jnp.broadcast_to(spin_sym[None, None], (quarter, 1, 2, WF, WF))
    spin_bloch = rotate(spin_ops, vectors)[:, 0]
    curvature, weighted = kubo(bloch_ops, spin_bloch, fermi_level)
    total_points = kcount * lax.axis_size("ka")
    partial_value = weighted.reshape(9, WF) / math.sqrt(total_points)
    totals = taken_together(taken_together(partial_value, "col"), "ka")
    band_out = jnp.transpose(curvature, (1, 2, 3, 0)).reshape(9, WF, quarter)
    return (band_out, totals)


def solution(mesh):
    in_specs = (
        P(("ka", "col"), None, None),
        P("ka", None, None, None),
        P(),
        P("ka", None),
        P(),
        P(),
        P(),
    )
    out_specs = (P(None, None, ("ka", "col")), P())
    return jax.shard_map(
        on_device, mesh=mesh, in_specs=in_specs, out_specs=out_specs, check_vma=False
    )
```

profile of v0, /device:TPU:1, one launch (start us, length us, event | category | flops | bytes accessed | tf_op | source)
XLA Modules:
  0.0 234.4 jit_solution(3155142561728896138)
XLA Ops:
  8.6 10.6 %all_to_all.44 = bf16[16,4,2304]{2,0,1:T(8,128)(2,1)} all-to-all(bf16[16,4,2304]{2,0,1:T(8,128)(2,1)S(1)} %copy.186), channel_id=1, replica_groups=mesh['ka'=32,'col'=4] {'col'}, dimensions={1} | all-to-all | bytes 589824 | tf_op jit(solution)/shard_map/all_to_all | solution.py:112
  22.6 8.6 %gather_fusion.1 = s32[2048]{0:T(1024)S(1)} fusion(s32[1024]{0:T(1024)S(1)} %copy-done.2, s32[2048]{0:T(1024)S(1)} %broadcast_clamp_fusion), kind=kCustom, calls=%fused_computation.1 | custom fusion | bytes 24576 | tf_op jit(solution)/shard_map/jit(_take)/gather | solution.py:29
  31.1 8.6 %gather_fusion = s32[2048,3]{1,0:T(8,128)} fusion(s32[1024,3]{1,0:T(8,128)} %copy.184, s32[2048]{0:T(1024)S(1)} %broadcast_clamp_fusion), kind=kCustom, calls=%fused_computation | custom fusion | bytes 57344 | tf_op jit(solution)/shard_map/jit(_take)/gather | solution.py:28
  44.5 3.5 %slice_reduce_fusion.2 = (f32[2048]{0:T(1024)S(1)}, f32[2048]{0:T(1024)S(1)}, f32[2048]{0:T(1024)S(1)}) fusion(f32[2048,3]{1,0:T(8,128)} %get-tuple-element.5), kind=kLoop, calls=%fused_computation.54 | loop fusion | bytes 49152 | tf_op jit(solution)/shard_map/slice | solution.py:39
  56.1 20.9 %all-gather.2.cloned.1.call-done = bf16[2048,2304]{1,0:T(8,128)(2,1)} async-done(((bf16[64,2304]{1,0:T(8,128)(2,1)}), bf16[2048,2304]{1,0:T(8,128)(2,1)}) %all-gather.2.cloned.1.call-update) | async-done | bytes 9437200 | tf_op jit(solution)/shard_map/all_gather | solution.py:113
  77.1 9.3 %fusion.2 = bf16[64,4,2,2304]{3,0,2,1:T(8,128)(2,1)S(1)} fusion(bf16[2048,2304]{1,0:T(8,128)(2,1)} %all-gather.2.cloned.1.call-done, bf16[64,4,1,2048]{3,0,2,1:T(8,128)(2,1)} %get-tuple-element.8, bf16[64,4,1,2048]{3,0,2,1:T(8,128)(2,1)} %get-tuple-element.7), kind=kOutput, calls=%fused_computation.5 | convolution fusion | flops 4834066432 | bytes 13893632 | tf_op jit(solution)/shard_map/dot_general | solution.py:117
  86.4 3.8 %copy.187 = bf16[64,4,2,2304]{3,2,1,0:T(2,128)(2,1)} copy(bf16[64,4,2,2304]{3,0,2,1:T(8,128)(2,1)S(1)} %fusion.2) | data formatting | bytes 4718592 | tf_op jit(solution)/shard_map/convert_element_type | solution.py:119
  90.2 4.7 %all-to-all-start.1 = ((bf16[64,4,2,2304]{3,2,1,0:T(2,128)(2,1)}), bf16[64,4,2,2304]{3,2,1,0:T(2,128)(2,1)}, u32[]{:S(2)}, u32[]{:S(2)}) async-start(bf16[64,4,2,2304]{3,2,1,0:T(2,128)(2,1)} %copy.187), calls=%async_computation.1 | async-start | bytes 4718592 | tf_op jit(solution)/shard_map/all_to_all | solution.py:120
  109.2 14.5 %all-to-all-done.1 = bf16[64,4,2,2304]{3,2,1,0:T(2,128)(2,1)} async-done(((bf16[64,4,2,2304]{3,2,1,0:T(2,128)(2,1)}), bf16[64,4,2,2304]{3,2,1,0:T(2,128)(2,1)}, u32[]{:S(2)}, u32[]{:S(2)}) %all-to-all-start.1) | async-done | bytes 2359328 | tf_op jit(solution)/shard_map/all_to_all | solution.py:120
  123.7 5.0 %copy.260 = bf16[4,16,4,2,2304]{4,0,2,1,3:T(4,128)(2,1)} copy(bf16[4,16,4,2,2304]{4,3,2,1,0:T(2,128)(2,1)} %bitcast.16) | data formatting | bytes 4718592 | tf_op jit(solution)/shard_map/all_to_all | solution.py:120
  128.7 7.4 %reshape.803 = bf16[16,4,2,96,96]{4,3,1,0,2:T(8,128)(2,1)} reshape(bf16[16,4,2,4,2304]{4,3,1,0,2:T(4,128)(2,1)} %bitcast.234) | data formatting | bytes 4718592 | tf_op jit(solution)/shard_map/reshape | solution.py:121
  145.9 3.6 %copy.192 = f32[16,4,96,96]{2,3,1,0:T(8,128)} copy(f32[16,4,96,96]{3,2,1,0:T(8,128)} %convolution_subtract_fusion) | data formatting | bytes 4718592 | tf_op jit(solution)/shard_map/sub | solution.py:71
  149.5 4.7 %convolution_add_fusion = f32[16,4,96,96]{3,2,1,0:T(8,128)} fusion(f32[16,4,96,96]{3,2,1,0:T(8,128)} %fusion.49, bf16[16,4,96,96]{3,2,1,0:T(8,128)(2,1)} %copy-done.10, bf16[64,2,96,96]{3,2,1,0:T(8,128)(2,1)S(1)} %copy-done, s32[]{:T(128)S(6)} %select_n.239, s32[]{:T(128)S(6)} %add.272), kind=kOutput, calls=%fused_computation.32 | convolution fusion | flops 113836032 | bytes 6291464 | tf_op jit(solution)/shard_map/kjn,kcjm->kcnm/dot_general | solution.py:70
  154.1 3.8 %copy.195 = f32[16,4,96,96]{3,2,1,0:T(8,128)} copy(f32[16,4,96,96]{2,3,1,0:T(8,128)} %bitcast.232) | data formatting | bytes 4718592 | tf_op jit(solution)/shard_map/add | solution.py:68
  157.9 5.3 %fusion.18 = (bf16[16,4,1,96,96]{4,3,1,0,2:T(8,128)(2,1)S(1)}, bf16[16,4,1,96,96]{4,3,1,0,2:T(8,128)(2,1)S(1)}) fusion(f32[16,4,96,96]{3,2,1,0:T(8,128)} %copy.195, f32[16,4,96,96]{3,2,1,0:T(8,128)} %convolution_add_fusion, f32[16,4,96,96]{3,2,1,0:T(8,128)S(1)} %copy-done.3, f32[16,4,96,96]{2,3,1,0:T(8,128)} %copy.192), kind=kLoop, calls=%fused_computation.36 | loop fusion | flops 3538944 | bytes 11796480 | tf_op jit(solution)/shard_map/stack | solution.py:76
  169.3 3.3 %fusion.12 = bf16[16,3,96,96]{3,2,1,0:T(8,128)(2,1)} fusion(f32[16,3,96,96]{3,2,1,0:T(8,128)S(1)} %convolution_subtract_fusion.1, f32[16,3,96,96]{2,3,1,0:T(8,128)} %copy.209), kind=kLoop, calls=%fused_computation.21 | loop fusion | flops 1327104 | bytes 4423680 | tf_op jit(solution)/shard_map/mul | solution.py:91
  175.2 3.1 %subtract_multiply_fusion = bf16[16,3,96,96]{3,2,1,0:T(8,128)(2,1)} fusion(f32[16,3,96,96]{3,2,1,0:T(8,128)} %copy.214, f32[16,3,96,96]{3,2,1,0:T(8,128)S(1)} %convolution_add_fusion.1), kind=kLoop, calls=%fused_computation.24 | loop fusion | flops 1327104 | bytes 4423680 | tf_op jit(solution)/shard_map/mul | solution.py:92
  178.3 4.0 %copy.196 = f32[16,96,96]{0,2,1:T(8,128)} copy(f32[16,96,96]{2,1,0:T(8,128)} %fusion.36) | data formatting | bytes 1179648 | tf_op jit(solution)/shard_map/convert_element_type | solution.py:80
  182.2 3.0 %gather_fusion.2 = f32[96,16]{1,0:T(8,128)S(1)} fusion(f32[16,96,96]{0,2,1:T(8,128)} %copy.196, s32[96]{0:T(128)S(1)} %or_bitcast_fusion), kind=kCustom, calls=%fused_computation.2 | custom fusion | bytes 13056 | tf_op jit(solution)/shard_map/jit(diagonal)/gather | solution.py:80
  190.4 3.9 %copy.210 = bf16[16,96,96,3]{2,3,1,0:T(4,128)(2,1)} copy(bf16[16,96,96,3]{1,2,3,0:T(8,128)(2,1)} %get-tuple-element.9) | data formatting | bytes 1769472 | tf_op jit(solution)/shard_map/kanm,kbmn,knm->kabn/dot_general | solution.py:96
  196.1 5.7 %fusion.5 = (f32[96,3,3]{1,2,0:T(4,128)S(1)}, f32[16,96,3,3]{3,2,1,0:T(4,128)}) fusion(f32[96,16]{0,1:T(8,128)S(1)} %divide_bitcast_fusion, f32[16,96,3,3]{3,2,1,0:T(4,128)S(1)} %fusion.8, bf16[16,96,96,3]{2,3,1,0:T(4,128)(2,1)S(1)} %copy-done.18, bf16[16,3,96,96]{3,2,1,0:T(8,128)(2,1)S(1)} %copy-done.19), kind=kOutput, calls=%fused_computation.7 | convolution fusion | flops 2708640 | bytes 1889664 | tf_op jit(solution)/shard_map/kanm,kbmn,knm->kabn/dot_general | solution.py:96
  202.0 6.5 %all_to_all.45 = f32[4,1,864]{2,1,0:T(1,128)S(1)} all-to-all(f32[4,1,864]{2,1,0:T(1,128)S(1)} %reshape.838), channel_id=1, replica_groups=mesh['ka'=32,'col'=4] {'col'}, dimensions={0} | all-to-all | bytes 27648 | tf_op jit(solution)/shard_map/all_to_all | solution.py:16
  210.7 7.7 %all-to-all-start.3 = ((f32[32,1,864]{2,1,0:T(1,128)}), f32[32,1,864]{2,1,0:T(1,128)S(1)}, u32[]{:S(2)}, u32[]{:S(2)}) async-start(f32[32,1,864]{2,1,0:T(1,128)} %reshape.840), calls=%async_computation.3 | async-start | bytes 229376 | tf_op jit(solution)/shard_map/all_to_all | solution.py:16
  221.3 4.6 %all-to-all-done.3 = f32[32,1,864]{2,1,0:T(1,128)S(1)} async-done(((f32[32,1,864]{2,1,0:T(1,128)}), f32[32,1,864]{2,1,0:T(1,128)S(1)}, u32[]{:S(2)}, u32[]{:S(2)}) %all-to-all-start.3) | async-done | bytes 110624 | tf_op jit(solution)/shard_map/all_to_all | solution.py:16
  (116 shorter events, 63.1 us)
Async XLA Ops:
  7.2 40.9 %copy-start = (bf16[64,2,96,96]{3,2,1,0:T(8,128)(2,1)S(1)}, bf16[64,2,96,96]{3,2,1,0:T(8,128)(2,1)}, u32[]{:S(2)}) copy-start(bf16[64,2,96,96]{3,2,1,0:T(8,128)(2,1)} %param.8) | copy-start | bytes 7077892
  7.2 15.4 %copy-start.2 = (s32[1024]{0:T(1024)S(1)}, s32[1024]{0:T(1024)}, u32[]{:S(2)}) copy-start(s32[1024]{0:T(1024)} %param.12) | copy-start | bytes 12292
  7.2 69.9 %all-gather.2.cloned.1.call-start = ((), (), s32[]{:S(2)}) async-start(), calls=%async_computation.4 | async-start | bytes 9732096 | tf_op jit(solution)/shard_map/all_gather | solution.py:113
  39.8 4.5 %copy-start.22 = (s32[64,3]{0,1:T(4,128)S(1)}, s32[64,3]{0,1:T(4,128)}, u32[]{:S(2)}) copy-start(s32[64,3]{0,1:T(4,128)} %param.10) | copy-start | bytes 2308
  48.0 4.3 %copy-start.20 = (bf16[96,96]{1,0:T(8,128)(2,1)}, bf16[96,96]{1,0:T(8,128)(2,1)S(1)}, u32[]{:S(2)}) copy-start(bf16[96,96]{1,0:T(8,128)(2,1)S(1)} %get-tuple-element.19) | copy-start | bytes 55300
  90.2 33.5 %all-to-all-start.1 = ((bf16[64,4,2,2304]{3,2,1,0:T(2,128)(2,1)}), bf16[64,4,2,2304]{3,2,1,0:T(2,128)(2,1)}, u32[]{:S(2)}, u32[]{:S(2)}) async-start(bf16[64,4,2,2304]{3,2,1,0:T(2,128)(2,1)} %copy.187), calls=%async_computation.1 | async-start | bytes 4718592 | tf_op jit(solution)/shard_map/all_to_all | solution.py:120
  94.9 2.9 %copy-start.16 = (f32[16,96,96]{2,1,0:T(8,128)S(1)}, f32[16,96,96]{2,1,0:T(8,128)}, u32[]{:S(2)}) copy-start(f32[16,96,96]{2,1,0:T(8,128)} %fusion.42) | copy-start | bytes 1769476
  106.1 3.0 %copy-start.12 = (f32[16,96,96]{2,1,0:T(8,128)S(1)}, f32[16,96,96]{2,1,0:T(8,128)}, u32[]{:S(2)}) copy-start(f32[16,96,96]{2,1,0:T(8,128)} %convolution_subtract_fusion.2) | copy-start | bytes 1769476
  106.1 3.0 %copy-start.17 = (f32[16,1,96,96]{3,2,0,1:T(8,128)S(1)}, f32[16,1,96,96]{3,2,0,1:T(8,128)}, u32[]{:S(2)}) copy-start(f32[16,1,96,96]{3,2,0,1:T(8,128)} %copy.207) | copy-start | bytes 1769476
  136.1 2.4 %copy-start.4 = (bf16[16,4,2,96,96]{4,3,1,0,2:T(8,128)(2,1)S(1)}, bf16[16,4,2,96,96]{4,3,1,0,2:T(8,128)(2,1)}, u32[]{:S(2)}) copy-start(bf16[16,4,2,96,96]{4,3,1,0,2:T(8,128)(2,1)} %reshape.803) | copy-start | bytes 7077892
  139.6 1.1 copy-start.10
  154.1 3.8 %copy-start.3 = (f32[16,4,96,96]{3,2,1,0:T(8,128)S(1)}, f32[16,4,96,96]{3,2,1,0:T(8,128)}, u32[]{:S(2)}) copy-start(f32[16,4,96,96]{3,2,1,0:T(8,128)} %convolution_subtract_fusion) | copy-start | bytes 7077892
  157.9 6.4 %copy-start.15 = (bf16[16,96,96,1]{2,1,3,0:T(8,128)(2,1)S(1)}, bf16[16,96,96,1]{2,1,3,0:T(8,128)(2,1)}, u32[]{:S(2)}) copy-start(bf16[16,96,96,1]{2,1,3,0:T(8,128)(2,1)} %fusion.34) | copy-start | bytes 884740
  163.2 1.6 copy-start.5
  163.2 3.6 %copy-start.8 = (bf16[16,4,1,96,96]{4,3,1,0,2:T(8,128)(2,1)}, bf16[16,4,1,96,96]{4,3,1,0,2:T(8,128)(2,1)S(1)}, u32[]{:S(2)}) copy-start(bf16[16,4,1,96,96]{4,3,1,0,2:T(8,128)(2,1)S(1)} %get-tuple-element.24) | copy-start | bytes 3538948
  169.3 3.4 %copy-start.6 = (bf16[16,4,1,96,96]{4,3,1,0,2:T(8,128)(2,1)S(1)}, bf16[16,4,1,96,96]{4,3,1,0,2:T(8,128)(2,1)}, u32[]{:S(2)}) copy-start(bf16[16,4,1,96,96]{4,3,1,0,2:T(8,128)(2,1)} %copy-done.5) | copy-start | bytes 3538948
  169.3 3.4 %copy-start.11 = (f32[16,3,96,96]{3,2,1,0:T(8,128)S(1)}, f32[16,3,96,96]{3,2,1,0:T(8,128)}, u32[]{:S(2)}) copy-start(f32[16,3,96,96]{3,2,1,0:T(8,128)} %fusion.25) | copy-start | bytes 5308420
  178.3 7.3 %copy-start.7 = (bf16[16,4,1,96,96]{4,3,1,0,2:T(8,128)(2,1)S(1)}, bf16[16,4,1,96,96]{4,3,1,0,2:T(8,128)(2,1)}, u32[]{:S(2)}) copy-start(bf16[16,4,1,96,96]{4,3,1,0,2:T(8,128)(2,1)} %copy-done.5) | copy-start | bytes 3538948
  178.3 7.3 %copy-start.9 = (bf16[16,4,1,96,96]{4,3,1,0,2:T(8,128)(2,1)S(1)}, bf16[16,4,1,96,96]{4,3,1,0,2:T(8,128)(2,1)}, u32[]{:S(2)}) copy-start(bf16[16,4,1,96,96]{4,3,1,0,2:T(8,128)(2,1)} %copy-done.8) | copy-start | bytes 3538948
  187.5 6.7 %copy-start.13 = (bf16[16,3,96,96]{3,2,1,0:T(8,128)(2,1)S(1)}, bf16[16,3,96,96]{3,2,1,0:T(8,128)(2,1)}, u32[]{:S(2)}) copy-start(bf16[16,3,96,96]{3,2,1,0:T(8,128)(2,1)} %subtract_multiply_fusion) | copy-start | bytes 2654212
  194.3 1.8 copy-start.18
  194.3 1.8 copy-start.19
  209.9 17.7 %copy-start.1 = (bf16[64,2,96,96]{3,2,1,0:T(8,128)(2,1)S(1)}, bf16[64,2,96,96]{3,2,1,0:T(8,128)(2,1)}, u32[]{:S(2)}) copy-start(bf16[64,2,96,96]{3,2,1,0:T(8,128)(2,1)} %param.8) | copy-start | bytes 7077892
  210.7 15.1 %all-to-all-start.3 = ((f32[32,1,864]{2,1,0:T(1,128)}), f32[32,1,864]{2,1,0:T(1,128)S(1)}, u32[]{:S(2)}, u32[]{:S(2)}) async-start(f32[32,1,864]{2,1,0:T(1,128)} %reshape.840), calls=%async_computation.3 | async-start | bytes 229376 | tf_op jit(solution)/shard_map/all_to_all | solution.py:16
  (2 other events, 1.4 us)
Sparse Core Ops, SparseCore 0:
  19.3 57.7 all-gather.1
where the time goes:
time: 236 us; the launch traced here: 234 us
  local copies, waits for them, and re-layouts  78.6 us (33%)
  matrix products  41.4 us (18%)
  waiting for transfers between devices  40.1 us (17%)
  other arithmetic  29.5 us (12%)
  blocking collectives  17.1 us (7%)
  between operations  15.3 us (6%)
  starting transfers between devices  12.4 us (5%)
    all_gather x1, waiting for transfers between devices, on_device(): segment = lax.all_gather(entry_slice, 'ka', axis=0, tiled=True)  20.9 us
    all_to_all x1, waiting for transfers between devices, on_device(): lax.all_to_all(own_entries, 'col', split_axis=0, concat_axis=3, tiled=True)  14.5 us
    all_to_all x1, blocking collectives, on_device(): lax.all_to_all(flat_shard, 'col', split_axis=1, concat_axis=0, tiled=True)  10.6 us
    dot_general x1, matrix products, on_device(): summed = jnp.dot(phases, segment, preferred_element_type=jnp.float32)  9.27 us
    gather x1, local copies, waits for them, and re-layouts, phase_rows(): lattice_rows = jnp.take(lattice, vector_index, axis=0)  8.64 us
    gather x1, local copies, waits for them, and re-layouts, phase_rows(): degree_rows = jnp.take(degrees, vector_index, axis=0)  8.58 us
    all_to_all x1, starting transfers between devices, sent_to_all(): return lax.all_to_all(copies, axis, split_axis=0, concat_axis=0, tiled=True)  7.66 us
    reshape x1, local copies, waits for them, and re-layouts, on_device(): interpolated = regrouped.reshape(quarter, 4, 2, WF, WF)  7.42 us
  transfers between devices with their start and end apart: 3, of which 3 were waited for; matrix products, arithmetic and copies ran while one was open for 22% of the time, Pallas kernels for 0%

commit v1 on v0

--- a/solution.py
+++ b/solution.py
@@ -109,7 +109,19 @@
     vectors = lax.dynamic_slice_in_dim(eigvecs, column * quarter, quarter, 0)
     flat_shard = hamiltonian.reshape(hamiltonian.shape[0] * 2, WF * WF)
     entry_width = WF * WF // col_count
-    entry_slice = lax.all_to_all(flat_shard, "col", split_axis=1, concat_axis=0, tiled=True)
+    ways, here = (lax.axis_size("col"), lax.axis_index("col"))
+    width = flat_shard.shape[1] // ways
+    shape = list(flat_shard.shape)
+    shape[1] = width
+    height_2 = shape[0]
+    shape[0] = height_2 * ways
+    full = jnp.zeros(shape, flat_shard.dtype)
+    for mask in range(ways):
+        part = lax.dynamic_slice_in_dim(flat_shard, (here ^ mask) * width, width, axis=1)
+        if mask:
+            part = lax.ppermute(part, "col", [(d, d ^ mask) for d in range(ways)])
+        full = lax.dynamic_update_slice_in_dim(full, part, (here ^ mask) * height_2, axis=0)
+    entry_slice = full
     segment = lax.all_gather(entry_slice, "ka", axis=0, tiled=True)
     height = segment.shape[0]
     phases = phase_rows(k_indices, r_vectors, degeneracy, height)

time: 236 us -> 239 us (1.013)
  blocking collectives: 17.1 us -> 6.54 us
  waiting for transfers between devices: 40.1 us -> 45 us
  starting transfers between devices: 12.4 us -> 16.8 us
  local copies, waits for them, and re-layouts: 78.6 us -> 82.6 us
    all_to_all x1 -> x0, blocking collectives: 10.6 us -> none  [on_device(): lax.all_to_all(flat_shard, 'col', split_axis=1, concat_axis=0, tiled=True)]
    ppermute x0 -> x3, starting transfers between devices: none -> 4.48 us  [on_device(): part = lax.ppermute(part, 'col', [(d, d ^ mask) for d in range(ways)])]
    ppermute x0 -> x3, waiting for transfers between devices: none -> 3.43 us  [on_device(): part = lax.ppermute(part, 'col', [(d, d ^ mask) for d in range(ways)])]
    dynamic_update_slice x0 -> x3, local copies, waits for them, and re-layouts: none -> 2.67 us  [on_device(): lax.dynamic_update_slice_in_dim(full, part, (here ^ mask) * height_2, axi...]
    unnamed x52 -> x58, local copies, waits for them, and re-layouts: 4.88 us -> 4.89 us
  transfers between devices with their start and end apart: 3 -> 6, of which waited for: 3 -> 5; matrix products, arithmetic and copies ran while one was open for 22% -> 22% of each run, Pallas kernels for 0% -> 0%
where the time goes in v1:
time: 239 us; the launch traced here: 237 us
  local copies, waits for them, and re-layouts  82.6 us (35%)
  waiting for transfers between devices  45 us (19%)
  matrix products  41.5 us (17%)
  other arithmetic  29.5 us (12%)
  starting transfers between devices  16.8 us (7%)
  between operations  15.3 us (6%)
  blocking collectives  6.54 us (3%)
    all_gather x1, waiting for transfers between devices, on_device(): segment = lax.all_gather(entry_slice, 'ka', axis=0, tiled=True)  22.5 us
    all_to_all x1, waiting for transfers between devices, on_device(): lax.all_to_all(own_entries, 'col', split_axis=0, concat_axis=3, tiled=True)  14.5 us
    dot_general x1, matrix products, on_device(): summed = jnp.dot(phases, segment, preferred_element_type=jnp.float32)  9.27 us
    gather x1, local copies, waits for them, and re-layouts, phase_rows(): lattice_rows = jnp.take(lattice, vector_index, axis=0)  8.61 us
    gather x1, local copies, waits for them, and re-layouts, phase_rows(): degree_rows = jnp.take(degrees, vector_index, axis=0)  8.58 us
    all_to_all x1, starting transfers between devices, sent_to_all(): return lax.all_to_all(copies, axis, split_axis=0, concat_axis=0, tiled=True)  7.65 us
    reshape x1, local copies, waits for them, and re-layouts, on_device(): interpolated = regrouped.reshape(quarter, 4, 2, WF, WF)  7.4 us
    all_to_all x1, blocking collectives, sent_to_all(): return lax.all_to_all(copies, axis, split_axis=0, concat_axis=0, tiled=True)  6.54 us
  transfers between devices with their start and end apart: 6, of which 5 were waited for; matrix products, arithmetic and copies ran while one was open for 22% of the time, Pallas kernels for 0%

profile of v1, /device:TPU:1, one launch (start us, length us, event | category | flops | bytes accessed | tf_op | source)
XLA Modules:
  0.0 237.3 jit_solution(4206747079253307424)
XLA Ops:
  24.2 8.6 %gather_fusion.1 = s32[2048]{0:T(1024)S(1)} fusion(s32[1024]{0:T(1024)S(1)} %copy-done.2, s32[2048]{0:T(1024)S(1)} %broadcast_clamp_fusion), kind=kCustom, calls=%fused_computation.1 | custom fusion | bytes 24576 | tf_op jit(solution)/shard_map/jit(_take)/gather | solution.py:29
  32.8 8.6 %gather_fusion = s32[2048,3]{1,0:T(8,128)} fusion(s32[1024,3]{1,0:T(8,128)} %copy.179, s32[2048]{0:T(1024)S(1)} %broadcast_clamp_fusion), kind=kCustom, calls=%fused_computation | custom fusion | bytes 57344 | tf_op jit(solution)/shard_map/jit(_take)/gather | solution.py:28
  46.0 3.4 %slice_reduce_fusion.2 = (f32[2048]{0:T(1024)S(1)}, f32[2048]{0:T(1024)S(1)}, f32[2048]{0:T(1024)S(1)}) fusion(f32[2048,3]{1,0:T(8,128)} %get-tuple-element.5), kind=kLoop, calls=%fused_computation.54 | loop fusion | bytes 49152 | tf_op jit(solution)/shard_map/slice | solution.py:39
  57.6 22.5 %all-gather.2.cloned.1.call-done = bf16[2048,2304]{1,0:T(8,128)(2,1)} async-done(((bf16[64,2304]{1,0:T(8,128)(2,1)}), bf16[2048,2304]{1,0:T(8,128)(2,1)}) %all-gather.2.cloned.1.call-update) | async-done | bytes 9437200 | tf_op jit(solution)/shard_map/all_gather | solution.py:125
  80.1 9.3 %fusion.2 = bf16[64,4,2,2304]{3,0,2,1:T(8,128)(2,1)S(1)} fusion(bf16[2048,2304]{1,0:T(8,128)(2,1)} %all-gather.2.cloned.1.call-done, bf16[64,4,1,2048]{3,0,2,1:T(8,128)(2,1)} %get-tuple-element.8, bf16[64,4,1,2048]{3,0,2,1:T(8,128)(2,1)} %get-tuple-element.7), kind=kOutput, calls=%fused_computation.5 | convolution fusion | flops 4834066432 | bytes 13893632 | tf_op jit(solution)/shard_map/dot_general | solution.py:129
  89.3 3.8 %copy.181 = bf16[64,4,2,2304]{3,2,1,0:T(2,128)(2,1)} copy(bf16[64,4,2,2304]{3,0,2,1:T(8,128)(2,1)S(1)} %fusion.2) | data formatting | bytes 4718592 | tf_op jit(solution)/shard_map/convert_element_type | solution.py:131
  93.2 4.7 %all-to-all-start = ((bf16[64,4,2,2304]{3,2,1,0:T(2,128)(2,1)}), bf16[64,4,2,2304]{3,2,1,0:T(2,128)(2,1)}, u32[]{:S(2)}, u32[]{:S(2)}) async-start(bf16[64,4,2,2304]{3,2,1,0:T(2,128)(2,1)} %copy.181), calls=%async_computation | async-start | bytes 4718592 | tf_op jit(solution)/shard_map/all_to_all | solution.py:132
  112.2 14.5 %all-to-all-done = bf16[64,4,2,2304]{3,2,1,0:T(2,128)(2,1)} async-done(((bf16[64,4,2,2304]{3,2,1,0:T(2,128)(2,1)}), bf16[64,4,2,2304]{3,2,1,0:T(2,128)(2,1)}, u32[]{:S(2)}, u32[]{:S(2)}) %all-to-all-start) | async-done | bytes 2359328 | tf_op jit(solution)/shard_map/all_to_all | solution.py:132
  126.7 5.0 %copy.254 = bf16[4,16,4,2,2304]{4,0,2,1,3:T(4,128)(2,1)} copy(bf16[4,16,4,2,2304]{4,3,2,1,0:T(2,128)(2,1)} %bitcast.14) | data formatting | bytes 4718592 | tf_op jit(solution)/shard_map/all_to_all | solution.py:132
  131.7 7.4 %reshape.802 = bf16[16,4,2,96,96]{4,3,1,0,2:T(8,128)(2,1)} reshape(bf16[16,4,2,4,2304]{4,3,1,0,2:T(4,128)(2,1)} %bitcast.231) | data formatting | bytes 4718592 | tf_op jit(solution)/shard_map/reshape | solution.py:133
  148.9 3.6 %copy.186 = f32[16,4,96,96]{2,3,1,0:T(8,128)} copy(f32[16,4,96,96]{3,2,1,0:T(8,128)} %convolution_subtract_fusion) | data formatting | bytes 4718592 | tf_op jit(solution)/shard_map/sub | solution.py:71
  152.5 4.7 %convolution_add_fusion = f32[16,4,96,96]{3,2,1,0:T(8,128)} fusion(f32[16,4,96,96]{3,2,1,0:T(8,128)} %fusion.49, bf16[16,4,96,96]{3,2,1,0:T(8,128)(2,1)} %copy-done.10, bf16[64,2,96,96]{3,2,1,0:T(8,128)(2,1)S(1)} %copy-done, s32[]{:T(128)S(6)} %select_n.262, s32[]{:T(128)S(6)} %add.301), kind=kOutput, calls=%fused_computation.32 | convolution fusion | flops 113836032 | bytes 6291464 | tf_op jit(solution)/shard_map/kjn,kcjm->kcnm/dot_general | solution.py:70
  157.2 3.8 %copy.189 = f32[16,4,96,96]{3,2,1,0:T(8,128)} copy(f32[16,4,96,96]{2,3,1,0:T(8,128)} %bitcast.229) | data formatting | bytes 4718592 | tf_op jit(solution)/shard_map/add | solution.py:68
  161.0 5.3 %fusion.18 = (bf16[16,4,1,96,96]{4,3,1,0,2:T(8,128)(2,1)S(1)}, bf16[16,4,1,96,96]{4,3,1,0,2:T(8,128)(2,1)S(1)}) fusion(f32[16,4,96,96]{3,2,1,0:T(8,128)} %copy.189, f32[16,4,96,96]{3,2,1,0:T(8,128)} %convolution_add_fusion, f32[16,4,96,96]{3,2,1,0:T(8,128)S(1)} %copy-done.3, f32[16,4,96,96]{2,3,1,0:T(8,128)} %copy.186), kind=kLoop, calls=%fused_computation.36 | loop fusion | flops 3538944 | bytes 11796480 | tf_op jit(solution)/shard_map/stack | solution.py:76
  172.4 3.3 %fusion.12 = bf16[16,3,96,96]{3,2,1,0:T(8,128)(2,1)} fusion(f32[16,3,96,96]{3,2,1,0:T(8,128)S(1)} %convolution_subtract_fusion.1, f32[16,3,96,96]{2,3,1,0:T(8,128)} %copy.203), kind=kLoop, calls=%fused_computation.21 | loop fusion | flops 1327104 | bytes 4423680 | tf_op jit(solution)/shard_map/mul | solution.py:91
  178.2 3.1 %subtract_multiply_fusion = bf16[16,3,96,96]{3,2,1,0:T(8,128)(2,1)} fusion(f32[16,3,96,96]{3,2,1,0:T(8,128)} %copy.208, f32[16,3,96,96]{3,2,1,0:T(8,128)S(1)} %convolution_add_fusion.1), kind=kLoop, calls=%fused_computation.24 | loop fusion | flops 1327104 | bytes 4423680 | tf_op jit(solution)/shard_map/mul | solution.py:92
  181.3 4.0 %copy.190 = f32[16,96,96]{0,2,1:T(8,128)} copy(f32[16,96,96]{2,1,0:T(8,128)} %fusion.36) | data formatting | bytes 1179648 | tf_op jit(solution)/shard_map/convert_element_type | solution.py:80
  185.3 2.9 %gather_fusion.2 = f32[96,16]{1,0:T(8,128)S(1)} fusion(f32[16,96,96]{0,2,1:T(8,128)} %copy.190, s32[96]{0:T(128)S(1)} %or_bitcast_fusion), kind=kCustom, calls=%fused_computation.2 | custom fusion | bytes 13056 | tf_op jit(solution)/shard_map/jit(diagonal)/gather | solution.py:80
  193.3 3.9 %copy.204 = bf16[16,96,96,3]{2,3,1,0:T(4,128)(2,1)} copy(bf16[16,96,96,3]{1,2,3,0:T(8,128)(2,1)} %get-tuple-element.9) | data formatting | bytes 1769472 | tf_op jit(solution)/shard_map/kanm,kbmn,knm->kabn/dot_general | solution.py:96
  199.0 5.7 %fusion.5 = (f32[96,3,3]{1,2,0:T(4,128)S(1)}, f32[16,96,3,3]{3,2,1,0:T(4,128)}) fusion(f32[96,16]{0,1:T(8,128)S(1)} %divide_bitcast_fusion, f32[16,96,3,3]{3,2,1,0:T(4,128)S(1)} %fusion.8, bf16[16,96,96,3]{2,3,1,0:T(4,128)(2,1)S(1)} %copy-done.18, bf16[16,3,96,96]{3,2,1,0:T(8,128)(2,1)S(1)} %copy-done.20), kind=kOutput, calls=%fused_computation.7 | convolution fusion | flops 2708640 | bytes 1889664 | tf_op jit(solution)/shard_map/kanm,kbmn,knm->kabn/dot_general | solution.py:96
  205.0 6.5 %all_to_all.25 = f32[4,1,864]{2,1,0:T(1,128)S(1)} all-to-all(f32[4,1,864]{2,1,0:T(1,128)S(1)} %reshape.837), channel_id=1, replica_groups=mesh['ka'=32,'col'=4] {'col'}, dimensions={0} | all-to-all | bytes 27648 | tf_op jit(solution)/shard_map/all_to_all | solution.py:16
  213.7 7.6 %all-to-all-start.2 = ((f32[32,1,864]{2,1,0:T(1,128)}), f32[32,1,864]{2,1,0:T(1,128)S(1)}, u32[]{:S(2)}, u32[]{:S(2)}) async-start(f32[32,1,864]{2,1,0:T(1,128)} %reshape.839), calls=%async_computation.2 | async-start | bytes 229376 | tf_op jit(solution)/shard_map/all_to_all | solution.py:16
  221.3 2.9 %copy.211 = f32[3,3,96,16]{2,3,1,0:T(8,128)} copy(f32[3,3,96,16]{0,1,2,3:T(4,128)} %bitcast.233) | data formatting | bytes 110592 | tf_op jit(solution)/shard_map/mul | solution.py:95
  224.2 4.6 %all-to-all-done.2 = f32[32,1,864]{2,1,0:T(1,128)S(1)} async-done(((f32[32,1,864]{2,1,0:T(1,128)}), f32[32,1,864]{2,1,0:T(1,128)S(1)}, u32[]{:S(2)}, u32[]{:S(2)}) %all-to-all-start.2) | async-done | bytes 110624 | tf_op jit(solution)/shard_map/all_to_all | solution.py:16
  (131 shorter events, 72.4 us)
Async XLA Ops:
  7.2 42.3 %copy-start = (bf16[64,2,96,96]{3,2,1,0:T(8,128)(2,1)S(1)}, bf16[64,2,96,96]{3,2,1,0:T(8,128)(2,1)}, u32[]{:S(2)}) copy-start(bf16[64,2,96,96]{3,2,1,0:T(8,128)(2,1)} %param.8) | copy-start | bytes 7077892
  7.2 15.9 %copy-start.23 = (bf16[2,96,96]{2,1,0:T(8,128)(2,1)S(1)}, bf16[2,96,96]{2,1,0:T(8,128)(2,1)}, u32[]{:S(2)}) copy-start(bf16[2,96,96]{2,1,0:T(8,128)(2,1)} %param.9) | copy-start | bytes 110596
  7.2 15.9 %copy-start.24 = (s32[1024,3]{0,1:T(4,128)S(1)}, s32[1024,3]{0,1:T(4,128)}, u32[]{:S(2)}) copy-start(s32[1024,3]{0,1:T(4,128)} %param.11) | copy-start | bytes 36868
  7.2 16.9 %copy-start.2 = (s32[1024]{0:T(1024)S(1)}, s32[1024]{0:T(1024)}, u32[]{:S(2)}) copy-start(s32[1024]{0:T(1024)} %param.12) | copy-start | bytes 12292
  7.2 72.9 %all-gather.2.cloned.1.call-start = ((), (), s32[]{:S(2)}) async-start(), calls=%async_computation.3 | async-start | bytes 9732096 | tf_op jit(solution)/shard_map/all_gather | solution.py:125
  10.9 4.5 %collective-permute-start = (bf16[16,2304]{1,0:T(8,128)(2,1)}, bf16[16,2304]{1,0:T(8,128)(2,1)}, u32[]{:S(2)}, u32[]{:S(2)}) collective-permute-start(bf16[16,2304]{1,0:T(8,128)(2,1)} %get-tuple-element.21), channel_id=1, source_target_pairs={{0,1},{1,0},{2,3},{3,2},{4,5},{5,4},{6,7},{7,6},{8,9},{9,8},{10,11... | collective-permute-start | bytes 221192 | tf_op jit(solution)/shard_map/ppermute | solution.py:122
  13.0 5.7 %collective-permute-start.1 = (bf16[16,2304]{1,0:T(8,128)(2,1)}, bf16[16,2304]{1,0:T(8,128)(2,1)}, u32[]{:S(2)}, u32[]{:S(2)}) collective-permute-start(bf16[16,2304]{1,0:T(8,128)(2,1)} %get-tuple-element.20), channel_id=1, source_target_pairs={{0,2},{1,3},{2,0},{3,1},{4,6},{5,7},{6,4},{7,5},{8,10},{9,11},{10,... | collective-permute-start | bytes 221192 | tf_op jit(solution)/shard_map/ppermute | solution.py:122
  15.4 5.2 %collective-permute-start.2 = (bf16[16,2304]{1,0:T(8,128)(2,1)}, bf16[16,2304]{1,0:T(8,128)(2,1)}, u32[]{:S(2)}, u32[]{:S(2)}) collective-permute-start(bf16[16,2304]{1,0:T(8,128)(2,1)} %get-tuple-element.19), channel_id=1, source_target_pairs={{0,3},{1,2},{2,1},{3,0},{4,7},{5,6},{6,5},{7,4},{8,11},{9,10},{10,... | collective-permute-start | bytes 221192 | tf_op jit(solution)/shard_map/ppermute | solution.py:122
  41.4 4.5 %copy-start.25 = (s32[64,3]{0,1:T(4,128)S(1)}, s32[64,3]{0,1:T(4,128)}, u32[]{:S(2)}) copy-start(s32[64,3]{0,1:T(4,128)} %param.10) | copy-start | bytes 2308
  49.5 4.3 %copy-start.21 = (bf16[96,96]{1,0:T(8,128)(2,1)}, bf16[96,96]{1,0:T(8,128)(2,1)S(1)}, u32[]{:S(2)}) copy-start(bf16[96,96]{1,0:T(8,128)(2,1)S(1)} %get-tuple-element.23) | copy-start | bytes 55300
  93.2 33.5 %all-to-all-start = ((bf16[64,4,2,2304]{3,2,1,0:T(2,128)(2,1)}), bf16[64,4,2,2304]{3,2,1,0:T(2,128)(2,1)}, u32[]{:S(2)}, u32[]{:S(2)}) async-start(bf16[64,4,2,2304]{3,2,1,0:T(2,128)(2,1)} %copy.181), calls=%async_computation | async-start | bytes 4718592 | tf_op jit(solution)/shard_map/all_to_all | solution.py:132
  97.9 2.9 %copy-start.16 = (f32[16,96,96]{2,1,0:T(8,128)S(1)}, f32[16,96,96]{2,1,0:T(8,128)}, u32[]{:S(2)}) copy-start(f32[16,96,96]{2,1,0:T(8,128)} %fusion.42) | copy-start | bytes 1769476
  109.1 3.0 %copy-start.12 = (f32[16,96,96]{2,1,0:T(8,128)S(1)}, f32[16,96,96]{2,1,0:T(8,128)}, u32[]{:S(2)}) copy-start(f32[16,96,96]{2,1,0:T(8,128)} %convolution_subtract_fusion.2) | copy-start | bytes 1769476
  109.1 3.0 %copy-start.17 = (f32[16,1,96,96]{3,2,0,1:T(8,128)S(1)}, f32[16,1,96,96]{3,2,0,1:T(8,128)}, u32[]{:S(2)}) copy-start(f32[16,1,96,96]{3,2,0,1:T(8,128)} %copy.201) | copy-start | bytes 1769476
  157.2 3.8 %copy-start.3 = (f32[16,4,96,96]{3,2,1,0:T(8,128)S(1)}, f32[16,4,96,96]{3,2,1,0:T(8,128)}, u32[]{:S(2)}) copy-start(f32[16,4,96,96]{3,2,1,0:T(8,128)} %convolution_subtract_fusion) | copy-start | bytes 7077892
  161.0 6.4 %copy-start.15 = (bf16[16,96,96,1]{2,1,3,0:T(8,128)(2,1)S(1)}, bf16[16,96,96,1]{2,1,3,0:T(8,128)(2,1)}, u32[]{:S(2)}) copy-start(bf16[16,96,96,1]{2,1,3,0:T(8,128)(2,1)} %fusion.34) | copy-start | bytes 884740
  166.3 3.5 %copy-start.8 = (bf16[16,4,1,96,96]{4,3,1,0,2:T(8,128)(2,1)}, bf16[16,4,1,96,96]{4,3,1,0,2:T(8,128)(2,1)S(1)}, u32[]{:S(2)}) copy-start(bf16[16,4,1,96,96]{4,3,1,0,2:T(8,128)(2,1)S(1)} %get-tuple-element.28) | copy-start | bytes 3538948
  172.4 3.4 %copy-start.6 = (bf16[16,4,1,96,96]{4,3,1,0,2:T(8,128)(2,1)S(1)}, bf16[16,4,1,96,96]{4,3,1,0,2:T(8,128)(2,1)}, u32[]{:S(2)}) copy-start(bf16[16,4,1,96,96]{4,3,1,0,2:T(8,128)(2,1)} %copy-done.5) | copy-start | bytes 3538948
  172.4 3.4 %copy-start.11 = (f32[16,3,96,96]{3,2,1,0:T(8,128)S(1)}, f32[16,3,96,96]{3,2,1,0:T(8,128)}, u32[]{:S(2)}) copy-start(f32[16,3,96,96]{3,2,1,0:T(8,128)} %fusion.25) | copy-start | bytes 5308420
  181.3 7.2 %copy-start.7 = (bf16[16,4,1,96,96]{4,3,1,0,2:T(8,128)(2,1)S(1)}, bf16[16,4,1,96,96]{4,3,1,0,2:T(8,128)(2,1)}, u32[]{:S(2)}) copy-start(bf16[16,4,1,96,96]{4,3,1,0,2:T(8,128)(2,1)} %copy-done.5) | copy-start | bytes 3538948
  181.3 7.2 %copy-start.9 = (bf16[16,4,1,96,96]{4,3,1,0,2:T(8,128)(2,1)S(1)}, bf16[16,4,1,96,96]{4,3,1,0,2:T(8,128)(2,1)}, u32[]{:S(2)}) copy-start(bf16[16,4,1,96,96]{4,3,1,0,2:T(8,128)(2,1)} %copy-done.8) | copy-start | bytes 3538948
  190.5 6.7 %copy-start.13 = (bf16[16,3,96,96]{3,2,1,0:T(8,128)(2,1)S(1)}, bf16[16,3,96,96]{3,2,1,0:T(8,128)(2,1)}, u32[]{:S(2)}) copy-start(bf16[16,3,96,96]{3,2,1,0:T(8,128)(2,1)} %subtract_multiply_fusion) | copy-start | bytes 2654212
  212.8 17.7 %copy-start.1 = (bf16[64,2,96,96]{3,2,1,0:T(8,128)(2,1)S(1)}, bf16[64,2,96,96]{3,2,1,0:T(8,128)(2,1)}, u32[]{:S(2)}) copy-start(bf16[64,2,96,96]{3,2,1,0:T(8,128)(2,1)} %param.8) | copy-start | bytes 7077892
  213.7 15.1 %all-to-all-start.2 = ((f32[32,1,864]{2,1,0:T(1,128)}), f32[32,1,864]{2,1,0:T(1,128)S(1)}, u32[]{:S(2)}, u32[]{:S(2)}) async-start(f32[32,1,864]{2,1,0:T(1,128)} %reshape.839), calls=%async_computation.2 | async-start | bytes 229376 | tf_op jit(solution)/shard_map/all_to_all | solution.py:16
  (8 other events, 10.8 us)
Sparse Core Ops, SparseCore 0:
  22.4 57.6 all-gather.1
